TPU v7x, 256 devices: a whole 4x4x8 slice. The times are simulated.
256 devices in a mesh: row: 16 (over z, y_lo), col: 16 (over x, y_hi, core).
Axes of the slice: x: 4, y: 4 (y_hi: 2, y_lo: 2; y = y_hi * 2 + y_lo), z: 8, core: 2. Of those that a mesh axis runs over, the one named last changes fastest.
Arguments:
- matrix: float32 [12288, 12288], P('row', 'col'), may hold values from -30 to 30
- panels: float32 [2, 12288, 256], P(None, ('col', 'row')), may hold values from -0.0546875 to 0.0546875
- factors: float32 [2, 256, 256], replicated, may hold values from -1 to 2, as said below
Outputs:
- reduced: float32 [12288, 12288], P('row', 'col')
Inputs may be any that keep to these rules, and one draw needn't show every extreme that they name: Each factors[s] is upper triangular with diagonal entries between 1 and 2.
All inputs are finite; a program needn't handle non-finite values.
Results may differ from a plain program's by a relative error of at most 0.0003.
Values sent between devices are 32-bit elements; how exact they have to be, the bound alone decides.
A program may use at most 64 MiB of HBM per device.

v0:
```python
import jax
import jax.numpy as jnp
from jax import lax
from jax.sharding import PartitionSpec as P

highest = lax.Precision.HIGHEST


def laid_out(tiles, dim):
    dims = list(tiles.shape[1:])
    dims[dim] *= tiles.shape[0]
    return jnp.moveaxis(tiles, 0, dim).reshape(dims)


def from_everyone(value, axis):
    copies = jnp.broadcast_to(value, (lax.axis_size(axis), *value.shape))
    return lax.all_to_all(copies, axis, split_axis=0, concat_axis=0, tiled=True)


def gathered_copies(value, axis, dim):
    return laid_out(from_everyone(value, axis), dim)


def padded_to(lines, peers):
    spare = -len(lines) % peers
    return jnp.pad(lines, [(0, spare)] + [(0, 0)] * (lines.ndim - 1))


def broadcast_by_parts(value, axis, root):
    lines = jnp.where(lax.axis_index(axis) == root, value, jnp.zeros_like(value)).reshape(
        -1, *value.shape[1:][-1:]
    )
    padded = padded_to(lines, lax.axis_size(axis))
    own = lax.psum_scatter(padded, axis, scatter_dimension=0, tiled=True)
    return lax.all_gather(own, axis, axis=0, tiled=True)[: len(lines)].reshape(value.shape)


def cut_along(value, dim, peers):
    before, after = (value.shape[:dim], value.shape[dim + 1 :])
    return jnp.moveaxis(value.reshape(*before, peers, -1, *after), dim, 0)


def sent_and_summed(value, axis, dim):
    tiles = cut_along(value, dim, lax.axis_size(axis))
    arrived = lax.all_to_all(tiles, axis, split_axis=0, concat_axis=0, tiled=True)
    return arrived.sum(axis=0)


def nested_sum(value, axes):
    lines = value.reshape(-1, value.shape[-1])
    own = sent_and_summed(padded_to(lines, lax.axis_size(axes)), axes, 0)
    whole = gathered_copies(own, axes, 0)
    return whole[: len(lines)].reshape(value.shape)


def matmul(left, right):
    return jnp.dot(left, right, precision=highest, preferred_element_type=jnp.float32)


def transposed_product(left, right):
    return lax.dot_general(
        left, right, (((0,), (0,)), ((), ())), precision=highest, preferred_element_type=jnp.float32
    )


def outer_product(left, right):
    return lax.dot_general(
        left, right, (((1,), (1,)), ((), ())), precision=highest, preferred_element_type=jnp.float32
    )


def per_device(matrix, panels, factors):
    row_count = lax.axis_size("row")
    col_count = lax.axis_size("col")
    my_row = lax.axis_index("row")
    block_rows = matrix.shape[0]
    share = panels.shape[1]
    source = my_row * col_count // row_count
    offset = share * (my_row * col_count - source * row_count)
    gathered = gathered_copies(panels, "row", 1)
    relayed = broadcast_by_parts(gathered, "col", source)
    current = matrix
    for section in range(panels.shape[0]):
        factor = factors[section]
        panel_cols = gathered[section]
        panel_rows = relayed[section]
        sums_rows = nested_sum(matmul(current, panel_cols), "col")
        sums_cols = nested_sum(transposed_product(current, panel_rows), "row")
        image_rows = matmul(sums_rows, factor)
        image_cols = matmul(sums_cols, factor)
        inner = nested_sum(transposed_product(panel_rows, image_rows), "row")
        correction = transposed_product(factor, inner)
        update_rows = image_rows - 0.5 * matmul(panel_rows, correction)
        update_cols = image_cols - 0.5 * matmul(panel_cols, correction)
        current = (
            current
            - outer_product(panel_rows, update_cols)
            - outer_product(update_rows, panel_cols)
        )
    return current


def solution(mesh):
    return jax.shard_map(
        per_device,
        mesh=mesh,
        in_specs=(P("row", "col"), P(None, ("col", "row"), None), P()),
        out_specs=P("row", "col"),
        check_vma=False,
    )
```

profile of v0, /device:TPU:2, one launch (start us, length us, event | category | flops | bytes accessed | tf_op | source)
XLA Modules:
  0.0 431.1 jit_solution(6263676906609410572)
XLA Ops:
  8.7 9.6 %all-to-all-start = ((f32[16,2,48,256]{3,2,1,0:T(8,128)}), f32[16,2,48,256]{3,2,1,0:T(8,128)S(1)}, u32[]{:S(2)}, u32[]{:S(2)}) async-start(f32[16,2,48,256]{3,2,1,0:T(8,128)} %broadcast_in_dim.24), calls=%async_computation | async-start | bytes 3145728 | tf_op jit(solution)/shard_map/all_to_all | solution.py:17
  18.4 39.6 %all-to-all-done = f32[16,2,48,256]{3,2,1,0:T(8,128)S(1)} async-done(((f32[16,2,48,256]{3,2,1,0:T(8,128)}), f32[16,2,48,256]{3,2,1,0:T(8,128)S(1)}, u32[]{:S(2)}, u32[]{:S(2)}) %all-to-all-start) | async-done | bytes 1572896 | tf_op jit(solution)/shard_map/all_to_all | solution.py:17
  59.3 73.6 %reduce-scatter.2.cloned.1.call-done = f32[96,256]{1,0:T(8,128)} async-done(((f32[1536,256]{1,0:T(8,128)}), f32[96,256]{1,0:T(8,128)}) %reduce-scatter.2.cloned.1.call-update) | async-done | bytes 98320 | tf_op jit(solution)/shard_map/reduce_scatter | solution.py:34
  137.0 18.4 %all_to_all.65 = f32[16,48,256]{2,1,0:T(8,128)S(1)} all-to-all(f32[16,48,256]{2,1,0:T(8,128)S(1)} %fusion.38), channel_id=1, replica_groups=mesh['row'=16,'col'=16] {'col'}, dimensions={0} | all-to-all | bytes 1572864 | tf_op jit(solution)/shard_map/all_to_all | solution.py:45
  155.6 17.7 %all_to_all.66 = f32[16,48,256]{2,1,0:T(8,128)S(1)} all-to-all(f32[16,48,256]{2,1,0:T(8,128)S(1)} %broadcast_in_dim.27), channel_id=1, replica_groups=mesh['row'=16,'col'=16] {'col'}, dimensions={0} | all-to-all | bytes 1572864 | tf_op jit(solution)/shard_map/all_to_all | solution.py:17
  175.0 13.4 %all-gather.2.cloned.1.call-done = f32[1536,256]{1,0:T(8,128)} async-done(((f32[96,256]{1,0:T(8,128)}), f32[1536,256]{1,0:T(8,128)}) %all-gather.2.cloned.1.call-update) | async-done | bytes 1572880 | tf_op jit(solution)/shard_map/all_gather | solution.py:35
  188.3 3.6 fusion.16
  191.9 7.1 %all-to-all-start.5 = ((f32[16,16,256]{2,1,0:T(8,128)}), f32[16,16,256]{2,1,0:T(8,128)S(1)}, u32[]{:S(2)}, u32[]{:S(2)}) async-start(f32[16,16,256]{2,1,0:T(8,128)} %bitcast.10), calls=%async_computation.6 | async-start | bytes 524288 | tf_op jit(solution)/shard_map/all_to_all | solution.py:45
  199.1 4.7 %convolution_bitcast_fusion = f32[768,256]{0,1:T(8,128)} fusion(f32[768,768]{1,0:T(8,128)} %param.3, f32[1536,256]{1,0:T(8,128)S(1)} %copy-done), kind=kOutput, calls=%fused_computation.3 | convolution fusion | flops 1811939328 | bytes 3932160 | tf_op jit(solution)/shard_map/dot_general | solution.py:61
  203.8 2.3 copy.9
  206.1 5.4 %all-to-all-done.5 = f32[16,16,256]{2,1,0:T(8,128)S(1)} async-done(((f32[16,16,256]{2,1,0:T(8,128)}), f32[16,16,256]{2,1,0:T(8,128)S(1)}, u32[]{:S(2)}, u32[]{:S(2)}) %all-to-all-start.5) | async-done | bytes 262176 | tf_op jit(solution)/shard_map/all_to_all | solution.py:45
  211.4 4.3 all-to-all-start.1
  215.8 22.5 %all-to-all-done.1 = f32[16,48,256]{2,1,0:T(8,128)} async-done(((f32[16,48,256]{2,1,0:T(8,128)}), f32[16,48,256]{2,1,0:T(8,128)}, u32[]{:S(2)}, u32[]{:S(2)}) %all-to-all-start.1) | async-done | bytes 786464 | tf_op jit(solution)/shard_map/all_to_all | solution.py:45
  239.0 3.5 all-to-all-start.6
  243.7 9.7 %all-to-all-done.6 = f32[16,16,256]{2,1,0:T(8,128)S(1)} async-done(((f32[16,16,256]{2,1,0:T(8,128)}), f32[16,16,256]{2,1,0:T(8,128)S(1)}, u32[]{:S(2)}, u32[]{:S(2)}) %all-to-all-start.6) | async-done | bytes 262176 | tf_op jit(solution)/shard_map/all_to_all | solution.py:17
  254.3 4.5 %all-to-all-start.2 = ((f32[16,48,256]{2,1,0:T(8,128)}), f32[16,48,256]{2,1,0:T(8,128)}, u32[]{:S(2)}, u32[]{:S(2)}) async-start(f32[16,48,256]{2,1,0:T(8,128)} %broadcast_in_dim.26), calls=%async_computation.3 | async-start | bytes 1572864 | tf_op jit(solution)/shard_map/all_to_all | solution.py:17
  260.5 2.8 fusion.3
  263.3 16.2 %all-to-all-done.2 = f32[16,48,256]{2,1,0:T(8,128)} async-done(((f32[16,48,256]{2,1,0:T(8,128)}), f32[16,48,256]{2,1,0:T(8,128)}, u32[]{:S(2)}, u32[]{:S(2)}) %all-to-all-start.2) | async-done | bytes 786464 | tf_op jit(solution)/shard_map/all_to_all | solution.py:17
  284.5 2.4 subtract_subtract_fusion.1
  289.0 18.5 %all_to_all.67 = f32[16,48,256]{2,1,0:T(8,128)} all-to-all(f32[16,48,256]{2,1,0:T(8,128)S(1)} %fusion.39), channel_id=1, replica_groups=mesh['row'=16,'col'=16] {'col'}, dimensions={0} | all-to-all | bytes 1572864 | tf_op jit(solution)/shard_map/all_to_all | solution.py:45
  308.8 17.5 %all_to_all.68 = f32[16,48,256]{2,1,0:T(8,128)S(1)} all-to-all(f32[16,48,256]{2,1,0:T(8,128)S(1)} %broadcast_in_dim.30), channel_id=1, replica_groups=mesh['row'=16,'col'=16] {'col'}, dimensions={0} | all-to-all | bytes 1572864 | tf_op jit(solution)/shard_map/all_to_all | solution.py:17
  329.2 3.5 all-to-all-start.11
  332.7 5.9 %fusion.11 = f32[768,256]{1,0:T(8,128)} fusion(f32[768,768]{1,0:T(8,128)S(1)} %subtract_subtract_fusion.1, f32[1536,256]{1,0:T(8,128)} %all-gather.2.cloned.1.call-done), kind=kOutput, calls=%fused_computation.20 | convolution fusion | flops 1811939328 | bytes 3932160 | tf_op jit(solution)/shard_map/dot_general | solution.py:61
  338.6 7.8 %all-to-all-done.11 = f32[16,16,256]{2,1,0:T(8,128)S(1)} async-done(((f32[16,16,256]{2,1,0:T(8,128)}), f32[16,16,256]{2,1,0:T(8,128)S(1)}, u32[]{:S(2)}, u32[]{:S(2)}) %all-to-all-start.11) | async-done | bytes 262176 | tf_op jit(solution)/shard_map/all_to_all | solution.py:45
  346.4 4.3 all-to-all-start.7
  350.7 22.9 %all-to-all-done.7 = f32[16,48,256]{2,1,0:T(8,128)} async-done(((f32[16,48,256]{2,1,0:T(8,128)}), f32[16,48,256]{2,1,0:T(8,128)}, u32[]{:S(2)}, u32[]{:S(2)}) %all-to-all-start.7) | async-done | bytes 786464 | tf_op jit(solution)/shard_map/all_to_all | solution.py:45
  374.3 3.5 all-to-all-start.12
  379.1 10.0 %all-to-all-done.12 = f32[16,16,256]{2,1,0:T(8,128)S(1)} async-done(((f32[16,16,256]{2,1,0:T(8,128)}), f32[16,16,256]{2,1,0:T(8,128)S(1)}, u32[]{:S(2)}, u32[]{:S(2)}) %all-to-all-start.12) | async-done | bytes 262176 | tf_op jit(solution)/shard_map/all_to_all | solution.py:17
  390.0 4.5 %all-to-all-start.8 = ((f32[16,48,256]{2,1,0:T(8,128)}), f32[16,48,256]{2,1,0:T(8,128)}, u32[]{:S(2)}, u32[]{:S(2)}) async-start(f32[16,48,256]{2,1,0:T(8,128)} %broadcast_in_dim.29), calls=%async_computation.9 | async-start | bytes 1572864 | tf_op jit(solution)/shard_map/all_to_all | solution.py:17
  396.2 3.1 fusion
  399.3 16.0 %all-to-all-done.8 = f32[16,48,256]{2,1,0:T(8,128)} async-done(((f32[16,48,256]{2,1,0:T(8,128)}), f32[16,48,256]{2,1,0:T(8,128)}, u32[]{:S(2)}, u32[]{:S(2)}) %all-to-all-start.8) | async-done | bytes 786464 | tf_op jit(solution)/shard_map/all_to_all | solution.py:17
  420.4 3.8 subtract_subtract_fusion
  (61 shorter events, 34.8 us)
Async XLA Ops:
  8.7 49.2 %all-to-all-start = ((f32[16,2,48,256]{3,2,1,0:T(8,128)}), f32[16,2,48,256]{3,2,1,0:T(8,128)S(1)}, u32[]{:S(2)}, u32[]{:S(2)}) async-start(f32[16,2,48,256]{3,2,1,0:T(8,128)} %broadcast_in_dim.24), calls=%async_computation | async-start | bytes 3145728 | tf_op jit(solution)/shard_map/all_to_all | solution.py:17
  18.3 114.6 %reduce-scatter.2.cloned.1.call-start = ((), (), s32[]{:S(2)}) async-start(), calls=%async_computation.14 | async-start | bytes 1671168 | tf_op jit(solution)/shard_map/reduce_scatter | solution.py:34
  59.3 129.1 %all-gather.2.cloned.1.call-start = ((), (), s32[]{:S(2)}) async-start(), calls=%async_computation.15 | async-start | bytes 1671168 | tf_op jit(solution)/shard_map/all_gather | solution.py:35
  133.0 2.0 copy-start.3
  133.2 148.3 %copy-start.5 = (f32[1,16,48,256]{3,2,1,0:T(8,128)}, f32[1,16,48,256]{3,2,1,0:T(8,128)S(1)}, u32[]{:S(2)}) copy-start(f32[1,16,48,256]{3,2,1,0:T(8,128)S(1)} %get-tuple-element.6) | copy-start | bytes 2359300
  137.0 36.3 %copy-start.8 = (f32[2,256,256]{2,1,0:T(8,128)S(1)}, f32[2,256,256]{2,1,0:T(8,128)}, u32[]{:S(2)}) copy-start(f32[2,256,256]{2,1,0:T(8,128)} %param.5) | copy-start | bytes 1572868
  188.3 10.7 %copy-start = (f32[1536,256]{1,0:T(8,128)S(1)}, f32[1536,256]{1,0:T(8,128)}, u32[]{:S(2)}) copy-start(f32[1536,256]{1,0:T(8,128)} %all-gather.2.cloned.1.call-done) | copy-start | bytes 4718596
  191.9 19.5 %all-to-all-start.5 = ((f32[16,16,256]{2,1,0:T(8,128)}), f32[16,16,256]{2,1,0:T(8,128)S(1)}, u32[]{:S(2)}, u32[]{:S(2)}) async-start(f32[16,16,256]{2,1,0:T(8,128)} %bitcast.10), calls=%async_computation.6 | async-start | bytes 524288 | tf_op jit(solution)/shard_map/all_to_all | solution.py:45
  211.4 26.8 %all-to-all-start.1 = ((f32[16,48,256]{2,1,0:T(8,128)}), f32[16,48,256]{2,1,0:T(8,128)}, u32[]{:S(2)}, u32[]{:S(2)}) async-start(f32[16,48,256]{2,1,0:T(8,128)} %bitcast.86), calls=%async_computation.2 | async-start | bytes 1572864 | tf_op jit(solution)/shard_map/all_to_all | solution.py:45
  239.0 14.4 %all-to-all-start.6 = ((f32[16,16,256]{2,1,0:T(8,128)}), f32[16,16,256]{2,1,0:T(8,128)S(1)}, u32[]{:S(2)}, u32[]{:S(2)}) async-start(f32[16,16,256]{2,1,0:T(8,128)} %broadcast_in_dim.28), calls=%async_computation.7 | async-start | bytes 524288 | tf_op jit(solution)/shard_map/all_to_all | solution.py:17
  253.4 5.5 %copy-start.13 = (f32[16,16,256]{2,1,0:T(8,128)}, f32[16,16,256]{2,1,0:T(8,128)S(1)}, u32[]{:S(2)}) copy-start(f32[16,16,256]{2,1,0:T(8,128)S(1)} %all-to-all-done.6) | copy-start | bytes 786436
  254.3 25.1 %all-to-all-start.2 = ((f32[16,48,256]{2,1,0:T(8,128)}), f32[16,48,256]{2,1,0:T(8,128)}, u32[]{:S(2)}, u32[]{:S(2)}) async-start(f32[16,48,256]{2,1,0:T(8,128)} %broadcast_in_dim.26), calls=%async_computation.3 | async-start | bytes 1572864 | tf_op jit(solution)/shard_map/all_to_all | solution.py:17
  282.3 2.2 copy-start.4
  282.3 2.2 copy-start.6
  282.3 2.2 copy-start.11
  308.7 17.6 %copy-start.9 = (f32[2,256,256]{2,1,0:T(8,128)S(1)}, f32[2,256,256]{2,1,0:T(8,128)}, u32[]{:S(2)}) copy-start(f32[2,256,256]{2,1,0:T(8,128)} %param.5) | copy-start | bytes 1572868
  308.7 18.3 %copy-start.1 = (f32[1536,256]{1,0:T(8,128)S(1)}, f32[1536,256]{1,0:T(8,128)}, u32[]{:S(2)}) copy-start(f32[1536,256]{1,0:T(8,128)} %all-gather.2.cloned.1.call-done) | copy-start | bytes 4718596
  327.1 2.1 copy-start.7
  329.2 17.2 %all-to-all-start.11 = ((f32[16,16,256]{2,1,0:T(8,128)}), f32[16,16,256]{2,1,0:T(8,128)S(1)}, u32[]{:S(2)}, u32[]{:S(2)}) async-start(f32[16,16,256]{2,1,0:T(8,128)} %bitcast.20), calls=%async_computation.12 | async-start | bytes 524288 | tf_op jit(solution)/shard_map/all_to_all | solution.py:45
  346.4 27.2 %all-to-all-start.7 = ((f32[16,48,256]{2,1,0:T(8,128)}), f32[16,48,256]{2,1,0:T(8,128)}, u32[]{:S(2)}, u32[]{:S(2)}) async-start(f32[16,48,256]{2,1,0:T(8,128)} %bitcast.87), calls=%async_computation.8 | async-start | bytes 1572864 | tf_op jit(solution)/shard_map/all_to_all | solution.py:45
  374.3 14.7 %all-to-all-start.12 = ((f32[16,16,256]{2,1,0:T(8,128)}), f32[16,16,256]{2,1,0:T(8,128)S(1)}, u32[]{:S(2)}, u32[]{:S(2)}) async-start(f32[16,16,256]{2,1,0:T(8,128)} %broadcast_in_dim.31), calls=%async_computation.13 | async-start | bytes 524288 | tf_op jit(solution)/shard_map/all_to_all | solution.py:17
  389.1 5.5 %copy-start.12 = (f32[16,16,256]{2,1,0:T(8,128)}, f32[16,16,256]{2,1,0:T(8,128)S(1)}, u32[]{:S(2)}) copy-start(f32[16,16,256]{2,1,0:T(8,128)S(1)} %all-to-all-done.12) | copy-start | bytes 786436
  390.0 25.3 %all-to-all-start.8 = ((f32[16,48,256]{2,1,0:T(8,128)}), f32[16,48,256]{2,1,0:T(8,128)}, u32[]{:S(2)}, u32[]{:S(2)}) async-start(f32[16,48,256]{2,1,0:T(8,128)} %broadcast_in_dim.29), calls=%async_computation.9 | async-start | bytes 1572864 | tf_op jit(solution)/shard_map/all_to_all | solution.py:17
  415.3 2.9 copy-start.2
  418.2 2.2 copy-start.10
Sparse Core Ops, SparseCore 0:
  59.4 73.4 reduce-scatter.1
  135.6 52.7 all-gather.1
where the time goes:
time: 433 us; the launch traced here: 431 us
  waiting for transfers between devices  237 us (55%)
  blocking collectives  72.1 us (17%)
  matrix products  48.2 us (11%)
  starting transfers between devices  45 us (10%)
  between operations  13.8 us (3%)
  local copies, waits for them, and re-layouts  10.1 us (2%)
  other arithmetic  4.93 us (1%)
    all_to_all x5, waiting for transfers between devices, from_everyone(): return lax.all_to_all(copies, axis, split_axis=0, concat_axis=0, tiled=True)  91.4 us
    reduce_scatter x1, waiting for transfers between devices, broadcast_by_parts(): own = lax.psum_scatter(padded, axis, scatter_dimension=0, tiled=True)  73.6 us
    all_to_all x4, waiting for transfers between devices, sent_and_summed(): lax.all_to_all(tiles, axis, split_axis=0, concat_axis=0, tiled=True)  58.5 us
    all_to_all x2, blocking collectives, sent_and_summed(): lax.all_to_all(tiles, axis, split_axis=0, concat_axis=0, tiled=True)  37 us
    all_to_all x2, blocking collectives, from_everyone(): return lax.all_to_all(copies, axis, split_axis=0, concat_axis=0, tiled=True)  35.2 us
    all_to_all x5, starting transfers between devices, from_everyone(): return lax.all_to_all(copies, axis, split_axis=0, concat_axis=0, tiled=True)  25.7 us
    dot_general x6, matrix products, transposed_product(): lax.dot_general(left, right, (((0,), (0,)), ((), ())), precision=highest,...  19.5 us
    all_to_all x4, starting transfers between devices, sent_and_summed(): lax.all_to_all(tiles, axis, split_axis=0, concat_axis=0, tiled=True)  19.2 us
  transfers between devices with their start and end apart: 11, of which 11 were waited for; matrix products, arithmetic and copies ran while one was open for 7% of the time, Pallas kernels for 0%

commit v1 on v0

--- a/solution.py
+++ b/solution.py
@@ -32,7 +32,9 @@
     )
     padded = padded_to(lines, lax.axis_size(axis))
     own = lax.psum_scatter(padded, axis, scatter_dimension=0, tiled=True)
-    return lax.all_gather(own, axis, axis=0, tiled=True)[: len(lines)].reshape(value.shape)
+    return jnp.concatenate(
+        lax.all_to_all(jnp.stack([own] * lax.axis_size(axis)), axis, 0, 0), axis=0
+    )[: len(lines)].reshape(value.shape)
 
 
 def cut_along(value, dim, peers):

time: 433 us -> 414 us (0.956)
  waiting for transfers between devices: 237 us -> 207 us
  local copies, waits for them, and re-layouts: 10.1 us -> 21.9 us
  starting transfers between devices: 45 us -> 56.7 us
  blocking collectives: 72.1 us -> 62.1 us
    reduce_scatter x1, waiting for transfers between devices: 73.6 us -> 29.8 us  [broadcast_by_parts(): own = lax.psum_scatter(padded, axis, scatter_dimension=0, tiled=True)]
    all_to_all x0 -> x1, waiting for transfers between devices: none -> 19 us  [broadcast_by_parts(): lax.all_to_all(jnp.stack([own] * lax.axis_size(axis)), axis, 0, 0)]
    all_to_all x2 -> x1, blocking collectives: 35.2 us -> 19.3 us  [from_everyone(): return lax.all_to_all(copies, axis, split_axis=0, concat_axis=0, tiled=True)]
    all_gather x1 -> x0, waiting for transfers between devices: 13.4 us -> none  [broadcast_by_parts(): lax.all_gather(own, axis, axis=0, tiled=True)[:len(lines)]]
    all_to_all x5 -> x6, waiting for transfers between devices: 91.4 us -> 103 us  [from_everyone(): return lax.all_to_all(copies, axis, split_axis=0, concat_axis=0, tiled=True)]
    all_to_all x5 -> x6, starting transfers between devices: 25.7 us -> 31.9 us  [from_everyone(): return lax.all_to_all(copies, axis, split_axis=0, concat_axis=0, tiled=True)]
    all_to_all x2, blocking collectives: 37 us -> 42.8 us  [sent_and_summed(): lax.all_to_all(tiles, axis, split_axis=0, concat_axis=0, tiled=True)]
    dot_general x1 -> x4, local copies, waits for them, and re-layouts: 2.29 us -> 7.68 us  [transposed_product(): lax.dot_general(left, right, (((0,), (0,)), ((), ())), precision=highest,...]
  transfers between devices with their start and end apart: 11 -> 12, of which waited for: 11 -> 12; matrix products, arithmetic and copies ran while one was open for 7% -> 7% of each run, Pallas kernels for 0% -> 0%
where the time goes in v1:
time: 414 us; the launch traced here: 413 us
  waiting for transfers between devices  207 us (50%)
  blocking collectives  62.1 us (15%)
  starting transfers between devices  56.7 us (14%)
  matrix products  45.1 us (11%)
  local copies, waits for them, and re-layouts  21.9 us (5%)
  between operations  13.8 us (3%)
  other arithmetic  6.06 us (1%)
    all_to_all x6, waiting for transfers between devices, from_everyone(): return lax.all_to_all(copies, axis, split_axis=0, concat_axis=0, tiled=True)  103 us
    all_to_all x4, waiting for transfers between devices, sent_and_summed(): lax.all_to_all(tiles, axis, split_axis=0, concat_axis=0, tiled=True)  54.8 us
    all_to_all x2, blocking collectives, sent_and_summed(): lax.all_to_all(tiles, axis, split_axis=0, concat_axis=0, tiled=True)  42.8 us
    all_to_all x6, starting transfers between devices, from_everyone(): return lax.all_to_all(copies, axis, split_axis=0, concat_axis=0, tiled=True)  31.9 us
    reduce_scatter x1, waiting for transfers between devices, broadcast_by_parts(): own = lax.psum_scatter(padded, axis, scatter_dimension=0, tiled=True)  29.8 us
    all_to_all x4, starting transfers between devices, sent_and_summed(): lax.all_to_all(tiles, axis, split_axis=0, concat_axis=0, tiled=True)  19.3 us
    all_to_all x1, blocking collectives, from_everyone(): return lax.all_to_all(copies, axis, split_axis=0, concat_axis=0, tiled=True)  19.3 us
    dot_general x10, matrix products, matmul(): jnp.dot(left, right, precision=highest, preferred_element_type=jnp.float32)  19.1 us
  transfers between devices with their start and end apart: 12, of which 12 were waited for; matrix products, arithmetic and copies ran while one was open for 7% of the time, Pallas kernels for 0%

profile of v1, /device:TPU:2, one launch (start us, length us, event | category | flops | bytes accessed | tf_op | source)
XLA Modules:
  0.0 412.7 jit_solution(9758662847050238990)
XLA Ops:
  8.7 9.6 %all-to-all-start = ((f32[16,2,48,256]{3,2,1,0:T(8,128)}), f32[16,2,48,256]{3,2,1,0:T(8,128)S(1)}, u32[]{:S(2)}, u32[]{:S(2)}) async-start(f32[16,2,48,256]{3,2,1,0:T(8,128)} %broadcast_in_dim.24), calls=%async_computation | async-start | bytes 3145728 | tf_op jit(solution)/shard_map/all_to_all | solution.py:17
  18.4 39.6 %all-to-all-done = f32[16,2,48,256]{3,2,1,0:T(8,128)S(1)} async-done(((f32[16,2,48,256]{3,2,1,0:T(8,128)}), f32[16,2,48,256]{3,2,1,0:T(8,128)S(1)}, u32[]{:S(2)}, u32[]{:S(2)}) %all-to-all-start) | async-done | bytes 1572896 | tf_op jit(solution)/shard_map/all_to_all | solution.py:17
  63.3 19.7 %all_to_all.70 = f32[16,48,256]{2,1,0:T(8,128)} all-to-all(f32[16,48,256]{2,1,0:T(8,128)S(1)} %fusion.30), channel_id=1, replica_groups=mesh['row'=16,'col'=16] {'col'}, dimensions={0} | all-to-all | bytes 1572864 | tf_op jit(solution)/shard_map/all_to_all | solution.py:47
  84.3 19.3 %all_to_all.71 = f32[16,48,256]{2,1,0:T(8,128)} all-to-all(f32[16,48,256]{2,1,0:T(8,128)S(1)} %broadcast_in_dim.27), channel_id=1, replica_groups=mesh['row'=16,'col'=16] {'col'}, dimensions={0} | all-to-all | bytes 1572864 | tf_op jit(solution)/shard_map/all_to_all | solution.py:17
  103.6 29.8 %reduce-scatter.2.cloned.1.call-done = f32[96,256]{1,0:T(8,128)} async-done(((f32[1536,256]{1,0:T(8,128)}), f32[96,256]{1,0:T(8,128)}) %reduce-scatter.2.cloned.1.call-update) | async-done | bytes 98320 | tf_op jit(solution)/shard_map/reduce_scatter | solution.py:34
  135.6 5.4 %all-to-all-start.1 = ((f32[16,96,256]{2,1,0:T(8,128)}), f32[16,96,256]{2,1,0:T(8,128)}, u32[]{:S(2)}, u32[]{:S(2)}) async-start(f32[16,96,256]{2,1,0:T(8,128)} %stack.2), calls=%async_computation.2 | async-start | bytes 3145728 | tf_op jit(solution)/shard_map/all_to_all | solution.py:36
  141.0 2.8 fusion.18
  143.8 19.0 %all-to-all-done.1 = f32[16,96,256]{2,1,0:T(8,128)} async-done(((f32[16,96,256]{2,1,0:T(8,128)}), f32[16,96,256]{2,1,0:T(8,128)}, u32[]{:S(2)}, u32[]{:S(2)}) %all-to-all-start.1) | async-done | bytes 1572896 | tf_op jit(solution)/shard_map/all_to_all | solution.py:36
  167.4 2.9 fusion.8
  170.3 7.2 %all-to-all-start.6 = ((f32[16,16,256]{2,1,0:T(8,128)}), f32[16,16,256]{2,1,0:T(8,128)S(1)}, u32[]{:S(2)}, u32[]{:S(2)}) async-start(f32[16,16,256]{2,1,0:T(8,128)} %fusion.8), calls=%async_computation.7 | async-start | bytes 524288 | tf_op jit(solution)/shard_map/all_to_all | solution.py:47
  177.6 4.2 %convolution_bitcast_fusion = f32[768,256]{0,1:T(8,128)} fusion(f32[768,256]{1,0:T(8,128)} %bitcast.103, f32[768,768]{1,0:T(8,128)S(1)} %copy-done), kind=kOutput, calls=%fused_computation.3 | convolution fusion | flops 1811939328 | bytes 3932160 | tf_op jit(solution)/shard_map/dot_general | solution.py:63
  184.0 5.1 %all-to-all-done.6 = f32[16,16,256]{2,1,0:T(8,128)S(1)} async-done(((f32[16,16,256]{2,1,0:T(8,128)}), f32[16,16,256]{2,1,0:T(8,128)S(1)}, u32[]{:S(2)}, u32[]{:S(2)}) %all-to-all-start.6) | async-done | bytes 262176 | tf_op jit(solution)/shard_map/all_to_all | solution.py:47
  189.1 4.3 %all-to-all-start.2 = ((f32[16,48,256]{2,1,0:T(8,128)}), f32[16,48,256]{2,1,0:T(8,128)}, u32[]{:S(2)}, u32[]{:S(2)}) async-start(f32[16,48,256]{2,1,0:T(8,128)} %bitcast.4), calls=%async_computation.3 | async-start | bytes 1572864 | tf_op jit(solution)/shard_map/all_to_all | solution.py:47
  193.5 21.1 %all-to-all-done.2 = f32[16,48,256]{2,1,0:T(8,128)} async-done(((f32[16,48,256]{2,1,0:T(8,128)}), f32[16,48,256]{2,1,0:T(8,128)}, u32[]{:S(2)}, u32[]{:S(2)}) %all-to-all-start.2) | async-done | bytes 786464 | tf_op jit(solution)/shard_map/all_to_all | solution.py:47
  215.4 3.5 all-to-all-start.7
  220.1 9.5 %all-to-all-done.7 = f32[16,16,256]{2,1,0:T(8,128)S(1)} async-done(((f32[16,16,256]{2,1,0:T(8,128)}), f32[16,16,256]{2,1,0:T(8,128)S(1)}, u32[]{:S(2)}, u32[]{:S(2)}) %all-to-all-start.7) | async-done | bytes 262176 | tf_op jit(solution)/shard_map/all_to_all | solution.py:17
  230.5 4.5 %all-to-all-start.3 = ((f32[16,48,256]{2,1,0:T(8,128)}), f32[16,48,256]{2,1,0:T(8,128)}, u32[]{:S(2)}, u32[]{:S(2)}) async-start(f32[16,48,256]{2,1,0:T(8,128)} %broadcast_in_dim.26), calls=%async_computation.4 | async-start | bytes 1572864 | tf_op jit(solution)/shard_map/all_to_all | solution.py:17
  237.3 17.3 %all-to-all-done.3 = f32[16,48,256]{2,1,0:T(8,128)} async-done(((f32[16,48,256]{2,1,0:T(8,128)}), f32[16,48,256]{2,1,0:T(8,128)}, u32[]{:S(2)}, u32[]{:S(2)}) %all-to-all-start.3) | async-done | bytes 786464 | tf_op jit(solution)/shard_map/all_to_all | solution.py:17
  264.2 23.1 %all_to_all.72 = f32[16,48,256]{2,1,0:T(8,128)} all-to-all(f32[16,48,256]{2,1,0:T(8,128)S(1)} %fusion.33), channel_id=1, replica_groups=mesh['row'=16,'col'=16] {'col'}, dimensions={0} | all-to-all | bytes 1572864 | tf_op jit(solution)/shard_map/all_to_all | solution.py:47
  289.4 6.3 %all-to-all-start.11 = ((f32[16,48,256]{2,1,0:T(8,128)}), f32[16,48,256]{2,1,0:T(8,128)}, u32[]{:S(2)}, u32[]{:S(2)}) async-start(f32[16,48,256]{2,1,0:T(8,128)} %broadcast_in_dim.30), calls=%async_computation.12 | async-start | bytes 1572864 | tf_op jit(solution)/shard_map/all_to_all | solution.py:17
  296.8 11.7 %all-to-all-done.11 = f32[16,48,256]{2,1,0:T(8,128)} async-done(((f32[16,48,256]{2,1,0:T(8,128)}), f32[16,48,256]{2,1,0:T(8,128)}, u32[]{:S(2)}, u32[]{:S(2)}) %all-to-all-start.11) | async-done | bytes 786464 | tf_op jit(solution)/shard_map/all_to_all | solution.py:17
  313.0 3.5 all-to-all-start.12
  318.5 4.6 %fusion.32 = f32[16,48,256]{2,1,0:T(8,128)} fusion(f32[16,48,768]{2,1,0:T(8,128)} %bitcast.112, f32[768,256,1]{1,0,2:T(8,128)S(1)} %bitcast.99), kind=kOutput, calls=%fused_computation.41 | convolution fusion | flops 1811939328 | bytes 3932160 | tf_op jit(solution)/shard_map/dot_general | solution.py:63
  323.0 6.4 %all-to-all-done.12 = f32[16,16,256]{2,1,0:T(8,128)S(1)} async-done(((f32[16,16,256]{2,1,0:T(8,128)}), f32[16,16,256]{2,1,0:T(8,128)S(1)}, u32[]{:S(2)}, u32[]{:S(2)}) %all-to-all-start.12) | async-done | bytes 262176 | tf_op jit(solution)/shard_map/all_to_all | solution.py:47
  329.5 4.3 %all-to-all-start.8 = ((f32[16,48,256]{2,1,0:T(8,128)}), f32[16,48,256]{2,1,0:T(8,128)}, u32[]{:S(2)}, u32[]{:S(2)}) async-start(f32[16,48,256]{2,1,0:T(8,128)} %fusion.32), calls=%async_computation.9 | async-start | bytes 1572864 | tf_op jit(solution)/shard_map/all_to_all | solution.py:47
  333.8 22.1 %all-to-all-done.8 = f32[16,48,256]{2,1,0:T(8,128)} async-done(((f32[16,48,256]{2,1,0:T(8,128)}), f32[16,48,256]{2,1,0:T(8,128)}, u32[]{:S(2)}, u32[]{:S(2)}) %all-to-all-start.8) | async-done | bytes 786464 | tf_op jit(solution)/shard_map/all_to_all | solution.py:47
  356.6 3.5 all-to-all-start.13
  361.4 9.9 %all-to-all-done.13 = f32[16,16,256]{2,1,0:T(8,128)S(1)} async-done(((f32[16,16,256]{2,1,0:T(8,128)}), f32[16,16,256]{2,1,0:T(8,128)S(1)}, u32[]{:S(2)}, u32[]{:S(2)}) %all-to-all-start.13) | async-done | bytes 262176 | tf_op jit(solution)/shard_map/all_to_all | solution.py:17
  372.2 4.5 %all-to-all-start.9 = ((f32[16,48,256]{2,1,0:T(8,128)}), f32[16,48,256]{2,1,0:T(8,128)}, u32[]{:S(2)}, u32[]{:S(2)}) async-start(f32[16,48,256]{2,1,0:T(8,128)} %broadcast_in_dim.29), calls=%async_computation.10 | async-start | bytes 1572864 | tf_op jit(solution)/shard_map/all_to_all | solution.py:17
  378.4 2.8 fusion
  381.2 15.7 %all-to-all-done.9 = f32[16,48,256]{2,1,0:T(8,128)} async-done(((f32[16,48,256]{2,1,0:T(8,128)}), f32[16,48,256]{2,1,0:T(8,128)}, u32[]{:S(2)}, u32[]{:S(2)}) %all-to-all-start.9) | async-done | bytes 786464 | tf_op jit(solution)/shard_map/all_to_all | solution.py:17
  402.0 3.8 subtract_subtract_fusion
  (70 shorter events, 52.0 us)
Async XLA Ops:
  8.7 49.2 %all-to-all-start = ((f32[16,2,48,256]{3,2,1,0:T(8,128)}), f32[16,2,48,256]{3,2,1,0:T(8,128)S(1)}, u32[]{:S(2)}, u32[]{:S(2)}) async-start(f32[16,2,48,256]{3,2,1,0:T(8,128)} %broadcast_in_dim.24), calls=%async_computation | async-start | bytes 3145728 | tf_op jit(solution)/shard_map/all_to_all | solution.py:17
  18.3 115.1 %reduce-scatter.2.cloned.1.call-start = ((), (), s32[]{:S(2)}) async-start(), calls=%async_computation.15 | async-start | bytes 1671168 | tf_op jit(solution)/shard_map/reduce_scatter | solution.py:34
  59.4 2.0 copy-start
  60.4 22.7 %copy-start.5 = (f32[1,16,48,256]{3,2,1,0:T(8,128)}, f32[1,16,48,256]{3,2,1,0:T(8,128)S(1)}, u32[]{:S(2)}) copy-start(f32[1,16,48,256]{3,2,1,0:T(8,128)S(1)} %get-tuple-element.6) | copy-start | bytes 2359300
  103.6 37.4 %copy-start.10 = (f32[2,256,256]{2,1,0:T(8,128)S(1)}, f32[2,256,256]{2,1,0:T(8,128)}, u32[]{:S(2)}) copy-start(f32[2,256,256]{2,1,0:T(8,128)} %param.5) | copy-start | bytes 1572868
  135.6 27.1 %all-to-all-start.1 = ((f32[16,96,256]{2,1,0:T(8,128)}), f32[16,96,256]{2,1,0:T(8,128)}, u32[]{:S(2)}, u32[]{:S(2)}) async-start(f32[16,96,256]{2,1,0:T(8,128)} %stack.2), calls=%async_computation.2 | async-start | bytes 3145728 | tf_op jit(solution)/shard_map/all_to_all | solution.py:36
  170.3 18.8 %all-to-all-start.6 = ((f32[16,16,256]{2,1,0:T(8,128)}), f32[16,16,256]{2,1,0:T(8,128)S(1)}, u32[]{:S(2)}, u32[]{:S(2)}) async-start(f32[16,16,256]{2,1,0:T(8,128)} %fusion.8), calls=%async_computation.7 | async-start | bytes 524288 | tf_op jit(solution)/shard_map/all_to_all | solution.py:47
  189.1 25.5 %all-to-all-start.2 = ((f32[16,48,256]{2,1,0:T(8,128)}), f32[16,48,256]{2,1,0:T(8,128)}, u32[]{:S(2)}, u32[]{:S(2)}) async-start(f32[16,48,256]{2,1,0:T(8,128)} %bitcast.4), calls=%async_computation.3 | async-start | bytes 1572864 | tf_op jit(solution)/shard_map/all_to_all | solution.py:47
  193.4 41.6 %copy-start.11 = (f32[2,256,256]{2,1,0:T(8,128)S(1)}, f32[2,256,256]{2,1,0:T(8,128)}, u32[]{:S(2)}) copy-start(f32[2,256,256]{2,1,0:T(8,128)} %param.5) | copy-start | bytes 1572868
  193.5 42.1 %copy-start.2 = (f32[8,96,256]{2,1,0:T(8,128)S(1)}, f32[8,96,256]{2,1,0:T(8,128)}, u32[]{:S(2)}) copy-start(f32[8,96,256]{2,1,0:T(8,128)} %get-tuple-element.8) | copy-start | bytes 2359300
  193.5 42.1 %copy-start.8 = (f32[768,256]{1,0:T(8,128)S(1)}, f32[768,256]{1,0:T(8,128)}, u32[]{:S(2)}) copy-start(f32[768,256]{1,0:T(8,128)} %fusion.18) | copy-start | bytes 2359300
  215.4 14.2 %all-to-all-start.7 = ((f32[16,16,256]{2,1,0:T(8,128)}), f32[16,16,256]{2,1,0:T(8,128)S(1)}, u32[]{:S(2)}, u32[]{:S(2)}) async-start(f32[16,16,256]{2,1,0:T(8,128)} %broadcast_in_dim.28), calls=%async_computation.8 | async-start | bytes 524288 | tf_op jit(solution)/shard_map/all_to_all | solution.py:17
  230.5 24.1 %all-to-all-start.3 = ((f32[16,48,256]{2,1,0:T(8,128)}), f32[16,48,256]{2,1,0:T(8,128)}, u32[]{:S(2)}, u32[]{:S(2)}) async-start(f32[16,48,256]{2,1,0:T(8,128)} %broadcast_in_dim.26), calls=%async_computation.4 | async-start | bytes 1572864 | tf_op jit(solution)/shard_map/all_to_all | solution.py:17
  235.6 21.0 %copy-start.6 = (f32[1,16,48,256]{3,2,1,0:T(8,128)S(1)}, f32[1,16,48,256]{3,2,1,0:T(8,128)}, u32[]{:S(2)}) copy-start(f32[1,16,48,256]{3,2,1,0:T(8,128)} %copy-done.5) | copy-start | bytes 2359300
  257.4 2.2 copy-start.1
  257.5 2.2 copy-start.7
  257.5 2.2 copy-start.14
  259.7 2.4 copy-start.3
  289.4 19.1 %all-to-all-start.11 = ((f32[16,48,256]{2,1,0:T(8,128)}), f32[16,48,256]{2,1,0:T(8,128)}, u32[]{:S(2)}, u32[]{:S(2)}) async-start(f32[16,48,256]{2,1,0:T(8,128)} %broadcast_in_dim.30), calls=%async_computation.12 | async-start | bytes 1572864 | tf_op jit(solution)/shard_map/all_to_all | solution.py:17
  308.5 2.9 copy-start.12
  310.6 0.9 copy-start.9
  313.0 16.5 %all-to-all-start.12 = ((f32[16,16,256]{2,1,0:T(8,128)}), f32[16,16,256]{2,1,0:T(8,128)S(1)}, u32[]{:S(2)}, u32[]{:S(2)}) async-start(f32[16,16,256]{2,1,0:T(8,128)} %fusion.6), calls=%async_computation.13 | async-start | bytes 524288 | tf_op jit(solution)/shard_map/all_to_all | solution.py:47
  329.5 26.4 %all-to-all-start.8 = ((f32[16,48,256]{2,1,0:T(8,128)}), f32[16,48,256]{2,1,0:T(8,128)}, u32[]{:S(2)}, u32[]{:S(2)}) async-start(f32[16,48,256]{2,1,0:T(8,128)} %fusion.32), calls=%async_computation.9 | async-start | bytes 1572864 | tf_op jit(solution)/shard_map/all_to_all | solution.py:47
  356.6 14.6 %all-to-all-start.13 = ((f32[16,16,256]{2,1,0:T(8,128)}), f32[16,16,256]{2,1,0:T(8,128)S(1)}, u32[]{:S(2)}, u32[]{:S(2)}) async-start(f32[16,16,256]{2,1,0:T(8,128)} %broadcast_in_dim.31), calls=%async_computation.14 | async-start | bytes 524288 | tf_op jit(solution)/shard_map/all_to_all | solution.py:17
  371.2 5.5 %copy-start.15 = (f32[16,16,256]{2,1,0:T(8,128)}, f32[16,16,256]{2,1,0:T(8,128)S(1)}, u32[]{:S(2)}) copy-start(f32[16,16,256]{2,1,0:T(8,128)S(1)} %all-to-all-done.13) | copy-start | bytes 786436
  372.2 24.7 %all-to-all-start.9 = ((f32[16,48,256]{2,1,0:T(8,128)}), f32[16,48,256]{2,1,0:T(8,128)}, u32[]{:S(2)}, u32[]{:S(2)}) async-start(f32[16,48,256]{2,1,0:T(8,128)} %broadcast_in_dim.29), calls=%async_computation.10 | async-start | bytes 1572864 | tf_op jit(solution)/shard_map/all_to_all | solution.py:17
  396.9 2.1 copy-start.4
  399.8 2.2 copy-start.13
Sparse Core Ops, SparseCore 0:
  59.4 74.0 reduce-scatter.1
